TPU v7x, 32 devices: a whole 2x2x4 slice. The times are simulated.
32 devices in a mesh: grp: 8 (over y, x, core), col: 4 (over z).
Axes of the slice: x: 2, y: 2, z: 4, core: 2. Of those that a mesh axis runs over, the one named last changes fastest.
Arguments:
- old_tables: bfloat16 [32, 128, 32768], P(('grp', 'col')), may hold values from -3 to 3
- table_rows: int32 [32], replicated, may hold values from 4096 to 32768, as said below
- old_plan: int32 [32], replicated, may hold values from 0 to 31, each once
- new_plan: int32 [32], replicated, may hold values from 0 to 31, each once
- ids: int32 [256, 32, 16], P(('grp', 'col')), may hold values from 0 to 32767, as said below
- bag_len: int32 [256, 32], P(('grp', 'col')), may hold values from 1 to 16
Outputs:
- new_tables: bfloat16 [32, 128, 32768], P('grp', 'col')
- pooled: float32 [256, 32, 128], P(('grp', 'col'))
Inputs may be any that keep to these rules, and one draw needn't show every extreme that they name: table_rows[t] is a multiple of 4096, and some table has exactly 32768 rows. `ids`: every id of table t lies below table_rows[t].
All inputs are finite; a program needn't handle non-finite values.
Results may differ from a plain program's by a relative error of at most 0.001.
Values may be sent and summed in bfloat16 or wider, within the bound.
A program may use at most 128 MiB of HBM per device.

v0:
```python
import functools

import jax
import jax.numpy as jnp
from jax import lax
from jax.experimental import pallas as pl
from jax.experimental.pallas import tpu as pltpu
from jax.sharding import PartitionSpec as P

UNIT = 4096
LANES = 128
KEYS = 256
NARROW = 16
MESH = pl.DeviceIdType.MESH
AHEAD = 3
WINDOW = 2
CHUNKS = 32
ORDER = (4, 2, 6, 3, 5, 7, 1)
VMEM_ROOM = 56 * 1024 * 1024
LAG = 2
SHARES = ((42, 38), (44, 42), (46, 46), (48, 50), (50, 54), (54, 60), (64, 64))


def chunk_list(unit, halves):
    chunks = []
    for start in range(0, unit, 8 * LANES):
        for half in range(halves):
            chunks.append((1, 4, half, start))
    return chunks


def move_kernel(shape, chunks, caps, old_ref, new_ref, table_ref, ids_ref, pick_ref, out_ref, pooled_ref, *scratch):
    groups, cols, units, width, per_group = shape
    count = len(chunks)
    spread, planes, gathered = scratch[:count], scratch[count : 2 * count], scratch[2 * count : 3 * count]
    (abuf, zbuf, cbuf, fbuf, a_send, a_recv, z_send, z_recv, c_send, c_recv, f_send, f_recv,
     own_ids, by_slot, held_ref, total, sums_ref, high_ref, low_ref, count_ref,
     i_send, i_recv, r_send, r_recv, t_sem) = scratch[3 * count :]
    g = lax.axis_index("grp")
    c = lax.axis_index("col")
    chip, core = g // 2, lax.rem(g, 2)
    chips = groups // 2
    cw = spread[0].shape[2]
    devices = groups * cols
    me = g * cols + c
    samples, tables, bag = ids_ref.shape
    slots, room = caps

    def aligned(value, unit):
        return pl.multiple_of(value * unit, unit)

    def place(k):
        stride, over, half, start = chunks[k]
        return stride, over, half, start, lax.rem(chip // stride, over)

    def spread_to(k, d):
        stride, over, half, start, mine = place(k)
        to_core = lax.rem(core + d // over, 2)
        to_part = lax.rem(mine + d % over, over)
        return to_core, to_part, (chip + (to_part - mine) * stride) * 2 + to_core

    def spread_step(k, d):
        stride, over, half, start, mine = place(k)
        slot = core * over + mine
        return pltpu.make_async_remote_copy(
            abuf.at[k % AHEAD, d], spread[k].at[pl.ds(slot * units, units)], a_send.at[k, d], a_recv.at[k, d],
            device_id=(spread_to(k, d)[2], c), device_id_type=MESH,
        )

    def spread_pack(k, d):
        stride, over, half, start, mine = place(k)
        slot = core * over + mine
        to_core, to_part, to = spread_to(k, d)
        block = start // LANES + to_core * over + to_part

        def step(e, carry):
            rows = pl.ds(aligned(e * (UNIT // LANES) + block, LANES), LANES)
            if d == 0:
                spread[k][slot * units + e] = held_ref[:, half, :, rows]
            else:
                abuf[k % AHEAD, d, e] = held_ref[:, half, :, rows]
            return carry

        lax.fori_loop(0, units, step, 0, unroll=2)

    def spread_first():
        stride, over, half, start, mine = place(0)
        slot = core * over + mine
        for d in list(range(1, 2 * over)) + [0]:
            to_core, to_part, to = spread_to(0, d)
            block = start // LANES + to_core * over + to_part

            def step(e, carry):
                src = table_ref.at[:, half, :, pl.ds(aligned(e * (UNIT // LANES) + block, LANES), LANES)]
                dst = spread[0].at[slot * units + e]
                if d == 0:
                    pltpu.make_async_copy(src, dst, a_recv.at[0, 0]).start()
                else:
                    pltpu.make_async_remote_copy(
                        src, dst, a_send.at[0, d], a_recv.at[0, d], device_id=(to, c), device_id_type=MESH
                    ).start()
                return carry

            lax.fori_loop(0, units, step, 0)

    def spread_start(k):
        others = range(1, 2 * chunks[k][1])
        if k >= AHEAD:
            for d in others:
                spread_step(k - AHEAD, d).wait_send()
        for d in others:
            spread_pack(k, d)
            spread_step(k, d).start()
        spread_pack(k, 0)

    def column_step(k, d):
        to = lax.rem(c + d, cols)
        return pltpu.make_async_remote_copy(
            zbuf.at[k % 2, to], planes[k].at[pl.ds(c * slots, slots)], z_send.at[k, d], z_recv.at[k, d],
            device_id=(g, to), device_id_type=MESH,
        )

    def chip_step(k, d):
        to = lax.rem(chip + d, chips)
        return pltpu.make_async_remote_copy(
            cbuf.at[k % 2, d], gathered[k].at[pl.ds(chip * room, room)], c_send.at[k, d], c_recv.at[k, d],
            device_id=(to * 2 + core, c), device_id_type=MESH,
        )

    def out_start(k):
        stride, over, half, start, mine = place(k)
        rows = over * LANES
        for d in (1, 0):

            def step(e, carry):
                src = fbuf.at[k % 2, d, e]
                dst = out_ref.at[
                    :, pl.ds(half * cw, cw),
                    pl.ds(aligned(e * (UNIT // LANES) + start // LANES + core * over, LANES), rows),
                ]
                if d == 0:
                    pltpu.make_async_copy(src, dst, f_recv.at[k, 0]).start()
                else:
                    pltpu.make_async_remote_copy(
                        src, dst, f_send.at[k], f_recv.at[k, 1],
                        device_id=(chip * 2 + lax.rem(core + 1, 2), c), device_id_type=MESH,
                    ).start()
                return carry

            lax.fori_loop(0, units, step, 0)

    def out_done(k, d):
        part = fbuf.at[k % 2, d]
        if d == 0:
            return pltpu.make_async_copy(part, part, f_recv.at[k, 0])
        return pltpu.make_async_remote_copy(
            part, part, f_send.at[k], f_recv.at[k, 1],
            device_id=(chip * 2 + lax.rem(core + 1, 2), c), device_id_type=MESH,
        )

    def ids_step(d):
        to = lax.rem(me + d, devices)
        src, dst = by_slot.at[to], own_ids.at[me]
        if isinstance(d, int):
            return pltpu.make_async_copy(src, dst, i_recv.at[d])
        return pltpu.make_async_remote_copy(
            src, dst, i_send.at[d], i_recv.at[d],
            device_id=(to // cols, lax.rem(to, cols)), device_id_type=MESH,
        )

    def sums_step(d):
        to = lax.rem(me + d, devices)
        src, dst = total.at[to], sums_ref.at[me]
        if isinstance(d, int):
            return pltpu.make_async_copy(src, dst, r_recv.at[d])
        return pltpu.make_async_remote_copy(
            src, dst, r_send.at[d], r_recv.at[d],
            device_id=(to // cols, lax.rem(to, cols)), device_id_type=MESH,
        )

    def each_peer(act):
        def step(d, carry):
            act(d)
            return carry

        lax.fori_loop(1, devices, step, 0)

    def fetch(e):
        rows = pl.ds(aligned(e, UNIT), UNIT)
        return pltpu.make_async_copy(table_ref.at[:, :, :, rows], held_ref.at[:, :, :, rows], t_sem.at[e])

    block, span = low_ref.shape[1] // bag, low_ref.shape[2]
    fold, blocks = block // samples, low_ref.shape[0]
    levels = units * UNIT // span // count

    def iota(shape, axis):
        return lax.broadcasted_iota(jnp.int32, shape, axis)

    def one_hot(same):
        return jnp.where(same, jnp.float32(1), jnp.float32(0)).astype(jnp.bfloat16)

    def digits(q, carry):
        keys = block * bag
        wanted = own_ids[pl.ds(q * fold, fold)].reshape(block, bag)
        high = lax.shift_right_arithmetic(wanted, span.bit_length() - 1).astype(jnp.float32)
        low = (wanted & (span - 1)).astype(jnp.float32)
        across = one_hot(lax.rem(iota((bag, keys), 1), bag) == iota((bag, keys), 0))
        spread_high = jnp.dot(high.astype(jnp.bfloat16), across, preferred_element_type=jnp.float32)
        own = iota((block, keys), 1) // bag == iota((block, keys), 0)
        high_ref[q] = jnp.where(own, spread_high, -1.0)
        down = one_hot(iota((keys, block), 0) // bag == iota((keys, block), 1))
        rows = jnp.dot(down, low.astype(jnp.bfloat16), preferred_element_type=jnp.float32)
        rows = jnp.where(lax.rem(iota((keys, bag), 0), bag) == iota((keys, bag), 1), rows, 0.0)
        ones = jnp.ones((bag, span), jnp.bfloat16)
        value = jnp.dot(rows.astype(jnp.bfloat16), ones, preferred_element_type=jnp.float32)
        low_ref[q] = one_hot(value == iota((keys, span), 1).astype(jnp.float32))
        return carry

    def count_rows(p):
        def one(q, carry):
            high = high_ref[q] - lax.convert_element_type(p * levels, jnp.float32)
            left = jnp.concatenate([one_hot(high == jnp.float32(h)) for h in range(levels)], axis=0)
            counts = jnp.dot(left, low_ref[q], preferred_element_type=jnp.float32)
            count_ref[:, pl.ds(aligned(q, block), block), :] = counts.astype(jnp.bfloat16).reshape(levels, block, span)
            return carry

        lax.fori_loop(0, blocks, one, 0)

    def pool(p):
        group = 4

        def one(h, carry):
            sums = None
            for i in range(group):
                level = h * group + i
                values = held_ref[:, :, :, pl.ds(aligned(p * levels + level, span), span)].reshape(width, span)
                term = lax.dot_general(
                    count_ref[level], values, (((1,), (1,)), ((), ())), preferred_element_type=jnp.float32
                )
                sums = term if sums is None else sums + term
            total[...] = total[...] + sums.reshape(devices, samples, width)
            return carry

        lax.fori_loop(0, levels // group, one, 0)

    def order_ids(s, carry):
        by_slot[s] = ids_ref[:, pl.ds(old_ref[s], 1), :].reshape(samples, bag)
        return carry

    c_base = slots
    f_base = slots + chips * room
    t_base = f_base + 2 * per_group * units

    def pack_columns(k):
        for d in range(1, 2 * chunks[k][1]):
            spread_step(k, d).wait_recv()
        if k == 0:
            part = spread[0].at[pl.ds(0, units)]
            pltpu.make_async_copy(part, part, a_recv.at[0, 0]).wait()
        if k >= 2:
            for d in range(1, cols):
                column_step(k - 2, d).wait_send()

        def one(n, carry):
            item = pick_ref[n]
            for z in range(cols):
                zbuf[k % 2, z, n] = spread[k][item, z]
            planes[k][c * slots + n] = spread[k][item, c]
            return carry

        lax.fori_loop(0, slots, one, 0)
        for d in COLUMN_ORDER(cols):
            column_step(k, d).start()

    def pack_chips(k):
        for d in range(1, cols):
            column_step(k, d).wait_recv()
        if k >= 2:
            for d in range(1, chips):
                chip_step(k - 2, d).wait_send()
        for d in list(range(1, chips)) + [0]:

            def one(m, carry):
                item = planes[k][pick_ref[c_base + d * room + m]]
                if d == 0:
                    gathered[k][chip * room + m] = item
                else:
                    cbuf[k % 2, d, m] = item
                return carry

            lax.fori_loop(0, room, one, 0, unroll=4)
            if d > 0:
                chip_step(k, d).start()

    def finish(k):
        stride, over, half, start, mine = place(k)
        for d in range(1, chips):
            chip_step(k, d).wait_recv()
        if k >= 2:
            out_done(k - 2, 0).wait()
            out_done(k - 2, 1).wait_send()
        for d in range(2):
            owner = lax.rem(core + d, 2)

            def one(e, carry):
                for j in range(per_group):
                    item = pick_ref[f_base + (owner * per_group + j) * units + e]
                    for b in range(over):
                        fbuf[k % 2, d, e, j, :, b * LANES : (b + 1) * LANES] = gathered[k][item + b * stride * room]
                return carry

            lax.fori_loop(0, units, one, 0)
        out_start(k)

    spread_first()
    for e in range(units):
        fetch(e).start()
    lax.fori_loop(0, tables, order_ids, 0)
    each_peer(lambda d: ids_step(d).start())
    ids_step(0).start()
    for e in range(units):
        fetch(e).wait()
    for k in range(1, min(AHEAD, count)):
        spread_start(k)
    total[...] = jnp.zeros_like(total)
    each_peer(lambda d: ids_step(d).wait_recv())
    ids_step(0).wait()
    lax.fori_loop(0, blocks, digits, 0)

    def at(t, k, act):
        @pl.when(t == k)
        def _():
            act()

    def step(t, carry):
        for k in range(count):

            def begin(k=k):
                pack_columns(k)
                if k + AHEAD < count:
                    spread_start(k + AHEAD)

            at(t, k, begin)

        @pl.when(t < count)
        def _():
            count_rows(t)

        for k in range(count):
            at(t, k + 1, functools.partial(pack_chips, k))

        @pl.when(t < count)
        def _():
            pool(t)

        @pl.when(t == count - 1)
        def _():
            each_peer(lambda d: sums_step(d).start())
            sums_step(0).start()

        for k in range(count - 1):
            at(t, k + LAG + 1, functools.partial(finish, k))
        return carry

    lax.fori_loop(0, count + LAG, step, 0)
    each_peer(lambda d: sums_step(d).wait())
    sums_step(0).wait()
    for t in range(tables):
        pooled_ref[:, t, :] = sums_ref[pick_ref[t_base + t]]
    each_peer(lambda d: ids_step(d).wait_send())
    for k in range(max(count - AHEAD, 0), count):
        for d in range(1, 2 * chunks[k][1]):
            spread_step(k, d).wait_send()
    for k in range(max(count - 2, 0), count):
        for d in range(1, cols):
            column_step(k, d).wait_send()
    finish(count - 1)
    for k in range(count):
        out_done(k, 1).wait_recv()
    for k in range(max(count - 2, 0), count):
        for d in range(1, chips):
            chip_step(k, d).wait_send()
        out_done(k, 0).wait()
        out_done(k, 1).wait_send()


def COLUMN_ORDER(cols):
    return [d for d in (2, 1, 3) if d < cols] + list(range(4, cols))


def move_tables(old_tables, old_plan, new_plan, marked, picks, groups, cols, chunks, caps):
    _, width, table_len = old_tables.shape
    narrow = width // cols
    halves = narrow // NARROW
    tables = old_plan.shape[0]
    per_group = tables // groups
    units = table_len // UNIT
    count = len(chunks)
    dtype = old_tables.dtype
    devices = groups * cols
    chips = groups // 2
    samples, _, bag = marked.shape
    slots, room = caps
    tile = (NARROW, LANES)
    over = max(chunk[1] for chunk in chunks)
    dma = pltpu.SemaphoreType.DMA
    view = old_tables.reshape(cols, halves, NARROW, table_len)
    return pl.pallas_call(
        functools.partial(move_kernel, (groups, cols, units, width, per_group), chunks, caps),
        out_shape=(
            jax.ShapeDtypeStruct((per_group, narrow, table_len), dtype),
            jax.ShapeDtypeStruct((samples, tables, width), jnp.float32),
        ),
        in_specs=[
            pl.BlockSpec(memory_space=pltpu.SMEM),
            pl.BlockSpec(memory_space=pltpu.SMEM),
            pl.BlockSpec(memory_space=pl.ANY),
            pl.BlockSpec(memory_space=pltpu.VMEM),
            pl.BlockSpec(memory_space=pltpu.SMEM),
        ],
        out_specs=(pl.BlockSpec(memory_space=pl.ANY), pl.BlockSpec(memory_space=pltpu.VMEM)),
        scratch_shapes=[pltpu.VMEM((2 * chunk[1] * units, cols) + tile, dtype) for chunk in chunks]
        + [pltpu.VMEM((cols * slots,) + tile, dtype)] * count
        + [pltpu.VMEM((chips * room,) + tile, dtype)] * count
        + [
            pltpu.VMEM((AHEAD, 2 * over, units, cols) + tile, dtype),
            pltpu.VMEM((2, cols, slots) + tile, dtype),
            pltpu.VMEM((2, chips, room) + tile, dtype),
            pltpu.VMEM((2, 2, units, per_group, NARROW, over * LANES), dtype),
            dma((count, 2 * over)), dma((count, 2 * over)),
            dma((count, cols)), dma((count, cols)),
            dma((count, chips)), dma((count, chips)),
            dma((count,)), dma((count, 2)),
            pltpu.VMEM((devices, samples, bag), marked.dtype),
            pltpu.VMEM((devices, samples, bag), marked.dtype),
            pltpu.VMEM((cols, halves, NARROW, table_len), dtype),
            pltpu.VMEM((devices, samples, width), jnp.float32),
            pltpu.VMEM((devices, samples, width), jnp.float32),
            pltpu.VMEM((devices * samples * bag // KEYS, KEYS // bag, KEYS), jnp.float32),
            pltpu.VMEM((devices * samples * bag // KEYS, KEYS, KEYS), jnp.bfloat16),
            pltpu.VMEM((table_len // KEYS // count, devices * samples, KEYS), jnp.bfloat16),
        ]
        + [dma((devices,))] * 4
        + [dma((units,))],
        compiler_params=pltpu.CompilerParams(
            has_side_effects=True, vmem_limit_bytes=60 * 1024 * 1024
        ),
    )(old_plan, new_plan, view, marked, picks)


def whole_kernel(groups, cols, chunks, old_ref, new_ref, table_ref, ids_ref, out_ref, pooled_ref, *scratch):
    zbufs, spreads, picks = scratch[:chunks], scratch[chunks : 2 * chunks], scratch[2 * chunks : 3 * chunks]
    z_send, z_recv, s_send, s_recv, p_send, p_recv = scratch[3 * chunks : 3 * chunks + 6]
    own_ids, by_slot, tabs, total, sums_ref, source_ref, inverse_ref = scratch[3 * chunks + 6 : 3 * chunks + 13]
    i_send, i_recv, r_send, r_recv, t_sem = scratch[3 * chunks + 13 :]
    g = lax.axis_index("grp")
    c = lax.axis_index("col")
    per_group, narrow, table_len = out_ref.shape
    chunk_rows = table_len // chunks
    sub = chunk_rows // groups

    def aligned(value, unit):
        return pl.multiple_of(value * unit, unit)

    def column_step(k, d):
        to = lax.rem(c + d, cols)
        src = table_ref.at[0, pl.ds(aligned(to, narrow), narrow), pl.ds(k * chunk_rows, chunk_rows)]
        dst = zbufs[k].at[c]
        if d == 0:
            return pltpu.make_async_copy(src, dst, z_recv.at[k, d])
        return pltpu.make_async_remote_copy(
            src, dst, z_send.at[k, d], z_recv.at[k, d], device_id=(g, to), device_id_type=MESH
        )

    def spread_step(k, d):
        to = lax.rem(g + d, groups)
        src = zbufs[k].at[:, :, pl.ds(aligned(to, sub), sub)]
        dst = spreads[k].at[pl.ds(g * cols, cols)]
        if d == 0:
            return pltpu.make_async_copy(src, dst, s_recv.at[k, d])
        return pltpu.make_async_remote_copy(
            src, dst, s_send.at[k, d], s_recv.at[k, d], device_id=(to, c), device_id_type=MESH
        )

    def group_step(k, d):
        to = lax.rem(g + d, groups)
        src = picks[k].at[pl.ds(to * per_group, per_group)]
        dst = out_ref.at[:, :, pl.ds(aligned(k * groups + g, sub), sub)]
        if d == 0:
            return pltpu.make_async_copy(src, dst, p_recv.at[k, d])
        return pltpu.make_async_remote_copy(
            src, dst, p_send.at[k, d], p_recv.at[k, d], device_id=(to, c), device_id_type=MESH
        )

    devices = groups * cols
    me = g * cols + c
    samples, tables, bag = ids_ref.shape

    def ids_step(d):
        to = lax.rem(me + d, devices)
        src, dst = by_slot.at[to], own_ids.at[me]
        if isinstance(d, int):
            return pltpu.make_async_copy(src, dst, i_recv.at[d])
        return pltpu.make_async_remote_copy(
            src, dst, i_send.at[d], i_recv.at[d],
            device_id=(to // cols, lax.rem(to, cols)), device_id_type=MESH,
        )

    def sums_step(d):
        to = lax.rem(me + d, devices)
        src, dst = total.at[to], sums_ref.at[me]
        if isinstance(d, int):
            return pltpu.make_async_copy(src, dst, r_recv.at[d])
        return pltpu.make_async_remote_copy(
            src, dst, r_send.at[d], r_recv.at[d],
            device_id=(to // cols, lax.rem(to, cols)), device_id_type=MESH,
        )

    def each_peer(act):
        def step(d, carry):
            act(d)
            return carry

        lax.fori_loop(1, devices, step, 0)

    def fetch(k):
        return pltpu.make_async_copy(
            table_ref.at[0, :, pl.ds(k * chunk_rows, chunk_rows)], tabs.at[k % 2], t_sem.at[k % 2]
        )

    tile = 512 if chunk_rows % 512 == 0 else 128
    fold = 8 if devices % 8 == 0 else 1

    def pool(k):
        fetch(k).wait()
        if k + 1 < chunks:
            fetch(k + 1).start()
        columns = chunk_rows // tile

        def piece(step, carry):
            block, part = step // columns, lax.rem(step, columns)
            rows = samples * fold
            wanted = own_ids[pl.ds(block * fold, fold)].reshape(rows, bag)
            row = lax.broadcasted_iota(jnp.int32, (rows, tile), 1) + (k * chunk_rows + part * tile)
            counts = jnp.zeros((rows, tile), jnp.float32)
            for i in range(bag):
                counts = jnp.where(wanted[:, i : i + 1] == row, counts + 1.0, counts)
            values = tabs[k % 2, :, pl.ds(aligned(part, tile), tile)]
            sums = lax.dot_general(
                counts.astype(values.dtype), values, (((1,), (1,)), ((), ())),
                preferred_element_type=jnp.float32,
            )
            where = pl.ds(block * fold, fold)
            total[where] = total[where] + sums.reshape(fold, samples, values.shape[0])
            return carry

        lax.fori_loop(0, devices // fold * columns, piece, 0)

    def finish(copy, d):
        if d == 0:
            copy.wait()
        else:
            copy.wait_recv()

    col_order = [d for d in (2, 1, 3) if d < cols] + list(range(4, cols)) + [0]
    grp_order = [d for d in ORDER if d < groups] + list(range(8, groups)) + [0]

    def order_ids(s, carry):
        by_slot[s] = ids_ref[:, pl.ds(old_ref[s], 1), :].reshape(samples, bag)
        return carry

    def locate(j, carry):
        wanted = new_ref[j]

        def look(s, found):
            held = old_ref[s]
            return jnp.where(held == wanted, s, found[0]), jnp.where(held == j, s, found[1])

        source_ref[j], inverse_ref[j] = lax.fori_loop(0, tables, look, (0, 0))
        return carry

    for k in range(min(WINDOW, chunks)):
        for d in col_order:
            column_step(k, d).start()
    fetch(0).start()
    lax.fori_loop(0, tables, order_ids, 0)
    lax.fori_loop(0, tables, locate, 0)
    each_peer(lambda d: ids_step(d).start())
    ids_step(0).start()
    total[...] = jnp.zeros_like(total)
    each_peer(lambda d: ids_step(d).wait_recv())
    ids_step(0).wait()

    def route(k):
        for d in grp_order:
            finish(spread_step(k, d), d)

        def pick(i, carry):
            picks[k][i] = spreads[k][source_ref[i]]
            return carry

        lax.fori_loop(0, groups * per_group, pick, 0)
        for d in grp_order:
            group_step(k, d).start()

    for k in range(chunks):
        for d in col_order:
            finish(column_step(k, d), d)
        for d in grp_order:
            spread_step(k, d).start()
        if k + WINDOW < chunks:
            for d in col_order:
                column_step(k + WINDOW, d).start()
        if k > 0:
            route(k - 1)
        pool(k)
    route(chunks - 1)
    each_peer(lambda d: sums_step(d).start())
    sums_step(0).start()
    for k in range(chunks):
        for d in grp_order:
            finish(group_step(k, d), d)
        for d in col_order:
            if d > 0:
                column_step(k, d).wait_send()
        for d in grp_order:
            if d > 0:
                spread_step(k, d).wait_send()
                group_step(k, d).wait_send()
    each_peer(lambda d: ids_step(d).wait_send())
    each_peer(lambda d: sums_step(d).wait())
    sums_step(0).wait()
    for t in range(tables):
        pooled_ref[:, t, :] = sums_ref[inverse_ref[t]]


def move_whole(old_tables, old_plan, new_plan, marked, groups, cols):
    _, width, table_len = old_tables.shape
    narrow = width // cols
    tables = old_plan.shape[0]
    per_group = tables // groups
    chunks = min(CHUNKS, table_len // (groups * 128))
    chunk_rows = table_len // chunks
    sub = chunk_rows // groups
    dtype = old_tables.dtype
    devices = groups * cols
    samples, _, bag = marked.shape
    sems = [
        pltpu.SemaphoreType.DMA((chunks, n)) for n in (cols, cols, groups, groups, groups, groups)
    ]
    return pl.pallas_call(
        functools.partial(whole_kernel, groups, cols, chunks),
        out_shape=(
            jax.ShapeDtypeStruct((per_group, narrow, table_len), dtype),
            jax.ShapeDtypeStruct((samples, tables, width), jnp.float32),
        ),
        in_specs=[
            pl.BlockSpec(memory_space=pltpu.SMEM),
            pl.BlockSpec(memory_space=pltpu.SMEM),
            pl.BlockSpec(memory_space=pl.ANY),
            pl.BlockSpec(memory_space=pltpu.VMEM),
        ],
        out_specs=(pl.BlockSpec(memory_space=pl.ANY), pl.BlockSpec(memory_space=pltpu.VMEM)),
        scratch_shapes=[pltpu.VMEM((cols, narrow, chunk_rows), dtype)] * chunks
        + [pltpu.VMEM((groups * cols, narrow, sub), dtype)] * chunks
        + [pltpu.VMEM((tables, narrow, sub), dtype)] * chunks
        + sems
        + [
            pltpu.VMEM((devices, samples, bag), marked.dtype),
            pltpu.VMEM((devices, samples, bag), marked.dtype),
            pltpu.VMEM((2, width, chunk_rows), dtype),
            pltpu.VMEM((devices, samples, width), jnp.float32),
            pltpu.VMEM((devices, samples, width), jnp.float32),
            pltpu.SMEM((tables,), jnp.int32),
            pltpu.SMEM((tables,), jnp.int32),
        ]
        + [pltpu.SemaphoreType.DMA((devices,))] * 4
        + [pltpu.SemaphoreType.DMA((2,))],
        compiler_params=pltpu.CompilerParams(
            has_side_effects=True, vmem_limit_bytes=48 * 1024 * 1024
        ),
    )(old_plan, new_plan, old_tables, marked)


def place_kernel(per_group, units, plan_ref, rows_ref, moved_ref, out_ref, zeros, held, in_sem, out_sem):
    own = lax.axis_index("grp") * per_group
    zeros[...] = jnp.zeros_like(zeros)

    def used(i):
        return lax.rem(i, units) * UNIT < rows_ref[plan_ref[own + i // units]]

    def window(ref, i):
        return ref.at[i // units, :, pl.ds(pl.multiple_of(lax.rem(i, units) * UNIT, UNIT), UNIT)]

    def load(i):
        return pltpu.make_async_copy(window(moved_ref, i), held.at[i], in_sem.at[i])

    def store(i, source):
        return pltpu.make_async_copy(source, window(out_ref, i), out_sem.at[i])

    def first(i, carry):
        @pl.when(used(i))
        def _():
            load(i).start()

        @pl.when(jnp.logical_not(used(i)))
        def _():
            store(i, zeros).start()

        return carry

    def second(i, carry):
        @pl.when(used(i))
        def _():
            load(i).wait()
            store(i, held.at[i]).start()

        return carry

    def third(i, carry):
        store(i, zeros).wait()
        return carry

    for step in (first, second, third):
        lax.fori_loop(0, per_group * units, step, 0)


def clear_unused(moved, new_plan, table_rows):
    per_group, narrow, table_len = moved.shape
    units = table_len // UNIT
    dma = pltpu.SemaphoreType.DMA((per_group * units,))
    return pl.pallas_call(
        functools.partial(place_kernel, per_group, units),
        out_shape=jax.ShapeDtypeStruct(moved.shape, moved.dtype),
        in_specs=[
            pl.BlockSpec(memory_space=pltpu.SMEM),
            pl.BlockSpec(memory_space=pltpu.SMEM),
            pl.BlockSpec(memory_space=pl.ANY),
        ],
        out_specs=pl.BlockSpec(memory_space=pl.ANY),
        scratch_shapes=[
            pltpu.VMEM((narrow, UNIT), moved.dtype),
            pltpu.VMEM((per_group * units, narrow, UNIT), moved.dtype),
            dma, dma,
        ],
    )(new_plan, table_rows, moved)


def vmem_bytes(chunks, units, cols, chips, samples, bag, caps):
    slots, room = caps
    tiles = sum(2 * chunk[1] * units * cols + cols * slots + chips * room for chunk in chunks)
    tiles += 2 * (AHEAD * chunks[0][1] * units * cols + cols * slots + chips * room) + 3 * 1024
    counts = KEYS * (samples * bag + units * UNIT // KEYS // len(chunks) * samples)
    return (tiles * NARROW * LANES + counts) * 2


def body(old_tables, table_rows, old_plan, new_plan, ids, bag_len):
    groups = lax.axis_size("grp")
    cols = lax.axis_size("col")
    tables = old_plan.shape[0]
    per_group = tables // groups
    _, width, table_len = old_tables.shape
    units = table_len // UNIT
    chips = groups // 2
    bag_iota = lax.broadcasted_iota(jnp.int32, (1, 1, ids.shape[2]), 2)
    marked = jnp.where(bag_iota < bag_len[:, :, None], ids, -1)
    chunks = chunk_list(UNIT, width // cols // NARROW)

    over = chunks[0][1]
    slot = jnp.arange(tables, dtype=jnp.int32)
    plane, group = slot % cols, slot // cols
    part, base = (group // 2) % over, group // 2 // over
    order = group % 2 * over + part
    held = jnp.sum(jnp.where(old_plan[:, None] == slot[None, :], table_rows[None, :], 0), axis=1) // UNIT
    position = jnp.sum(jnp.where(old_plan[:, None] == new_plan[None, :], slot[None, :], 0), axis=1)
    target = position // per_group // 2
    slot_of = jnp.sum(jnp.where(old_plan[None, :] == slot[:, None], slot[None, :], 0), axis=1)
    same = base[:, None] == base[None, :]
    same_plane = plane[:, None] == plane[None, :]
    first = order[None, :] < order[:, None]
    z_off = jnp.sum(jnp.where(same & same_plane & first, held[None, :], 0), axis=1)
    ahead = (plane[None, :] < plane[:, None]) | (same_plane & first)
    c_off = jnp.sum(jnp.where(same & (target[:, None] == target[None, :]) & ahead, held[None, :], 0), axis=1)
    z_need, c_need = z_off + held, c_off + held

    g = lax.axis_index("grp")
    c = lax.axis_index("col")
    chip = g // 2

    def variant(caps):
        slots, room = caps

        def run(old_tables, old_plan, new_plan, marked):
            mine = base == chip // over
            n = jnp.arange(slots, dtype=jnp.int32)[:, None]
            inside = (mine & (plane == c))[None, :] & (n >= z_off[None, :]) & (n < (z_off + held)[None, :])
            z_pick = jnp.sum(jnp.where(inside, (order * units - z_off)[None, :] + n, 0), axis=1)
            m = jnp.arange(chips * room, dtype=jnp.int32)[:, None]
            to, m = (chip + m // room) % chips, m % room
            inside = mine[None, :] & (target[None, :] == to) & (m >= c_off[None, :]) & (m < (c_off + held)[None, :])
            c_pick = jnp.sum(jnp.where(inside, (plane * slots + z_off - c_off)[None, :] + m, 0), axis=1)
            f = jnp.arange(2 * per_group * units, dtype=jnp.int32)[:, None]
            where, e = chip * 2 * per_group + f // units, f % units
            inside = (position[None, :] == where) & (e < held[None, :])
            f_pick = jnp.sum(jnp.where(inside, (base * over * room + c_off)[None, :] + e, 0), axis=1)
            picks = jnp.concatenate([z_pick, c_pick, f_pick, slot_of])
            return move_tables(old_tables, old_plan, new_plan, marked, picks, groups, cols, chunks, caps)

        return run

    full = 2 * over * units
    room_full = 2 * per_group * units
    caps = [(full * a // 64, room_full * b // 64) for a, b in SHARES]
    caps = [cap for cap in caps if vmem_bytes(chunks, units, cols, chips, ids.shape[0] * groups * cols, ids.shape[2], cap) < VMEM_ROOM]
    branches = [variant(cap) for cap in caps]
    if not caps or caps[-1][0] < full:

        def fallback(old_tables, old_plan, new_plan, marked):
            return move_whole(old_tables, old_plan, new_plan, marked, groups, cols)

        branches.append(fallback)
    misfits = (((z_need > cap[0]) | (c_need > cap[1])).astype(jnp.int32) for cap in caps[: len(branches) - 1])
    level = jnp.max(sum(misfits, start=jnp.zeros_like(z_need)))
    moved, pooled = lax.switch(level, branches, old_tables, old_plan, new_plan, marked)
    return (clear_unused(moved, new_plan, table_rows), pooled)


def solution(mesh):
    return jax.shard_map(
        body,
        mesh=mesh,
        in_specs=(
            P(("grp", "col"), None, None),
            P(),
            P(),
            P(),
            P(("grp", "col"), None, None),
            P(("grp", "col"), None),
        ),
        out_specs=(P("grp", "col", None), P(("grp", "col"), None, None)),
        check_vma=False,
    )
```

profile of v0, /device:TPU:9, one launch (start us, length us, event | category | flops | bytes accessed | tf_op | source)
XLA Modules:
  0.0 192.5 jit_solution(6502644495942828814)
XLA Ops:
  0.7 0.9 select_reduce_fusion.21
  1.7 0.2 select_reduce_fusion.24
  1.9 0.7 fusion.59
  3.2 0.9 copy.9
  4.1 0.8 fusion.49
  4.9 179.9 %conditional.1 = ((bf16[4,32,32768]{2,1,0:T(8,128)(2,1)}, f32[8,32,128]{2,1,0:T(8,128)S(1)})) conditional(s32[]{:T(128)} %clamp.3, (bf16[1,128,32768]{2,1,0:T(8,128)(2,1)}, s32[]{:T(128)}, s32[32]{0:T(128)S(1)}, s32[]{:T(128)}, s32[32]{0:T(128)S(1)}, /*index=5*/s32[32]{0:T(128)S(1)}, s32[32]{0:T(128)S(1)}, ...), branch_computations={%region_6.10_spmd, %region_10.14_spmd, %region_14.18_spmd, %region... | conditional | flops 108720 | bytes 13242 | solution.py:824
  5.0 0.1 select_reduce_fusion.7
  5.1 0.1 select_reduce_fusion.6
  5.2 0.1 select_reduce_fusion.8
  5.3 0.7 pad_add_fusion.2.pick_ref
  6.0 178.3 %branch_2_fun.1 = (bf16[4,32,32768]{2,1,0:T(8,128)(2,1)}, f32[8,32,128]{2,1,0:T(8,128)S(1)}) custom-call(s32[32]{0:T(128)} %get-tuple-element.258.old_ref, s32[32]{0:T(128)} %get-tuple-element.259.new_ref, bf16[4,2,16,32768]{3,2,1,0:T(8,128)(2,1)} %bitcast.9, s32[8,32,16]{2,1,0:T(8,128)S(1)} %get-tuple-element.261.ids_ref, s32[326]{0:T(512)} %pad_add_fusion.2.pick_ref), custom_call_target="tpu_custom_call" | custom-call | tf_op jit(solution)/shard_map/cond/branch_2_fun/pallas_call | solution.py:408
  184.8 7.0 %shard_map.77 = bf16[4,32,32768]{2,1,0:T(8,128)(2,1)} custom-call(s32[32]{0:T(128)} %plan_ref.1, s32[32]{0:T(128)} %rows_ref.1, bf16[4,32,32768]{2,1,0:T(8,128)(2,1)} %get-tuple-element.347.moved_ref), custom_call_target="tpu_custom_call" | custom-call | tf_op jit(solution)/shard_map/pallas_call | solution.py:732
  191.8 0.7 copy.25
  (7 shorter events, 0.1 us)
where the time goes:
time: 193 us; the launch traced here: 192 us
  Pallas kernels  185 us (96%)
  other arithmetic  3.64 us (2%)
    pallas_call x1, Pallas kernels, move_tables(): pl.pallas_call(functools.partial(move_kernel, (groups, cols, units, width...  178 us
    pallas_call x1, Pallas kernels, clear_unused(): pl.pallas_call(functools.partial(place_kernel, per_group, units), out_sha...  6.99 us

commit v1 on v0

--- a/solution.py
+++ b/solution.py
@@ -83,25 +83,15 @@
 
         lax.fori_loop(0, units, step, 0, unroll=2)
 
-    def spread_first():
-        stride, over, half, start, mine = place(0)
-        slot = core * over + mine
-        for d in list(range(1, 2 * over)) + [0]:
-            to_core, to_part, to = spread_to(0, d)
-            block = start // LANES + to_core * over + to_part
-
-            def step(e, carry):
-                src = table_ref.at[:, half, :, pl.ds(aligned(e * (UNIT // LANES) + block, LANES), LANES)]
-                dst = spread[0].at[slot * units + e]
-                if d == 0:
-                    pltpu.make_async_copy(src, dst, a_recv.at[0, 0]).start()
-                else:
-                    pltpu.make_async_remote_copy(
-                        src, dst, a_send.at[0, d], a_recv.at[0, d], device_id=(to, c), device_id_type=MESH
-                    ).start()
-                return carry
-
-            lax.fori_loop(0, units, step, 0)
+    def greet(barrier):
+        def signal(d, carry):
+            to = lax.rem(me + d, devices)
+            pl.semaphore_signal(
+                barrier, inc=1, device_id=(to // cols, lax.rem(to, cols)), device_id_type=MESH
+            )
+            return carry
+
+        lax.fori_loop(1, devices, signal, 0)
 
     def spread_start(k):
         others = range(1, 2 * chunks[k][1])
@@ -127,27 +117,20 @@
             device_id=(to * 2 + core, c), device_id_type=MESH,
         )
 
-    def out_start(k):
+    def out_start(k, d, e):
         stride, over, half, start, mine = place(k)
-        rows = over * LANES
-        for d in (1, 0):
-
-            def step(e, carry):
-                src = fbuf.at[k % 2, d, e]
-                dst = out_ref.at[
-                    :, pl.ds(half * cw, cw),
-                    pl.ds(aligned(e * (UNIT // LANES) + start // LANES + core * over, LANES), rows),
-                ]
-                if d == 0:
-                    pltpu.make_async_copy(src, dst, f_recv.at[k, 0]).start()
-                else:
-                    pltpu.make_async_remote_copy(
-                        src, dst, f_send.at[k], f_recv.at[k, 1],
-                        device_id=(chip * 2 + lax.rem(core + 1, 2), c), device_id_type=MESH,
-                    ).start()
-                return carry
-
-            lax.fori_loop(0, units, step, 0)
+        src = fbuf.at[k % 2, d, e]
+        dst = out_ref.at[
+            :, pl.ds(half * cw, cw),
+            pl.ds(aligned(e * (UNIT // LANES) + start // LANES + core * over, LANES), over * LANES),
+        ]
+        if d == 0:
+            pltpu.make_async_copy(src, dst, f_recv.at[k, 0]).start()
+        else:
+            pltpu.make_async_remote_copy(
+                src, dst, f_send.at[k], f_recv.at[k, 1],
+                device_id=(chip * 2 + lax.rem(core + 1, 2), c), device_id_type=MESH,
+            ).start()
 
     def out_done(k, d):
         part = fbuf.at[k % 2, d]
@@ -254,9 +237,6 @@
     def pack_columns(k):
         for d in range(1, 2 * chunks[k][1]):
             spread_step(k, d).wait_recv()
-        if k == 0:
-            part = spread[0].at[pl.ds(0, units)]
-            pltpu.make_async_copy(part, part, a_recv.at[0, 0]).wait()
         if k >= 2:
             for d in range(1, cols):
                 column_step(k - 2, d).wait_send()
@@ -299,7 +279,7 @@
         if k >= 2:
             out_done(k - 2, 0).wait()
             out_done(k - 2, 1).wait_send()
-        for d in range(2):
+        for d in (1, 0):
             owner = lax.rem(core + d, 2)
 
             def one(e, carry):
@@ -307,19 +287,25 @@
                     item = pick_ref[f_base + (owner * per_group + j) * units + e]
                     for b in range(over):
                         fbuf[k % 2, d, e, j, :, b * LANES : (b + 1) * LANES] = gathered[k][item + b * stride * room]
+                out_start(k, d, e)
                 return carry
 
             lax.fori_loop(0, units, one, 0)
-        out_start(k)
-
-    spread_first()
+
+    barrier = pltpu.get_barrier_semaphore()
+    greet(barrier)
     for e in range(units):
         fetch(e).start()
     lax.fori_loop(0, tables, order_ids, 0)
+    for e in range(units):
+        fetch(e).wait()
+    for d in range(2 * chunks[0][1]):
+        spread_pack(0, d)
+    pl.semaphore_wait(barrier, devices - 1)
+    for d in range(1, 2 * chunks[0][1]):
+        spread_step(0, d).start()
     each_peer(lambda d: ids_step(d).start())
     ids_step(0).start()
-    for e in range(units):
-        fetch(e).wait()
     for k in range(1, min(AHEAD, count)):
         spread_start(k)
     total[...] = jnp.zeros_like(total)
@@ -388,7 +374,7 @@
     return [d for d in (2, 1, 3) if d < cols] + list(range(4, cols))
 
 
-def move_tables(old_tables, old_plan, new_plan, marked, picks, groups, cols, chunks, caps):
+def move_tables(old_tables, old_plan, new_plan, marked, picks, groups, cols, chunks, caps, number):
     _, width, table_len = old_tables.shape
     narrow = width // cols
     halves = narrow // NARROW
@@ -408,7 +394,7 @@
     return pl.pallas_call(
         functools.partial(move_kernel, (groups, cols, units, width, per_group), chunks, caps),
         out_shape=(
-            jax.ShapeDtypeStruct((per_group, narrow, table_len), dtype),
+            pltpu.VMEM((per_group, narrow, table_len), dtype),
             jax.ShapeDtypeStruct((samples, tables, width), jnp.float32),
         ),
         in_specs=[
@@ -418,7 +404,7 @@
             pl.BlockSpec(memory_space=pltpu.VMEM),
             pl.BlockSpec(memory_space=pltpu.SMEM),
         ],
-        out_specs=(pl.BlockSpec(memory_space=pl.ANY), pl.BlockSpec(memory_space=pltpu.VMEM)),
+        out_specs=(pl.BlockSpec(memory_space=pltpu.VMEM), pl.BlockSpec(memory_space=pltpu.VMEM)),
         scratch_shapes=[pltpu.VMEM((2 * chunk[1] * units, cols) + tile, dtype) for chunk in chunks]
         + [pltpu.VMEM((cols * slots,) + tile, dtype)] * count
         + [pltpu.VMEM((chips * room,) + tile, dtype)] * count
@@ -443,7 +429,7 @@
         + [dma((devices,))] * 4
         + [dma((units,))],
         compiler_params=pltpu.CompilerParams(
-            has_side_effects=True, vmem_limit_bytes=60 * 1024 * 1024
+            has_side_effects=True, collective_id=number, vmem_limit_bytes=54 * 1024 * 1024
         ),
     )(old_plan, new_plan, view, marked, picks)
 
@@ -682,7 +668,7 @@
     )(old_plan, new_plan, old_tables, marked)
 
 
-def place_kernel(per_group, units, plan_ref, rows_ref, moved_ref, out_ref, zeros, held, in_sem, out_sem):
+def place_kernel(per_group, units, plan_ref, rows_ref, moved_ref, out_ref, zeros, out_sem):
     own = lax.axis_index("grp") * per_group
     zeros[...] = jnp.zeros_like(zeros)
 
@@ -691,9 +677,6 @@
 
     def window(ref, i):
         return ref.at[i // units, :, pl.ds(pl.multiple_of(lax.rem(i, units) * UNIT, UNIT), UNIT)]
-
-    def load(i):
-        return pltpu.make_async_copy(window(moved_ref, i), held.at[i], in_sem.at[i])
 
     def store(i, source):
         return pltpu.make_async_copy(source, window(out_ref, i), out_sem.at[i])
@@ -701,7 +684,7 @@
     def first(i, carry):
         @pl.when(used(i))
         def _():
-            load(i).start()
+            store(i, window(moved_ref, i)).start()
 
         @pl.when(jnp.logical_not(used(i)))
         def _():
@@ -709,19 +692,11 @@
 
         return carry
 
-    def second(i, carry):
-        @pl.when(used(i))
-        def _():
-            load(i).wait()
-            store(i, held.at[i]).start()
-
-        return carry
-
     def third(i, carry):
         store(i, zeros).wait()
         return carry
 
-    for step in (first, second, third):
+    for step in (first, third):
         lax.fori_loop(0, per_group * units, step, 0)
 
 
@@ -731,18 +706,15 @@
     dma = pltpu.SemaphoreType.DMA((per_group * units,))
     return pl.pallas_call(
         functools.partial(place_kernel, per_group, units),
-        out_shape=jax.ShapeDtypeStruct(moved.shape, moved.dtype),
+        out_shape=pltpu.HBM(moved.shape, moved.dtype),
         in_specs=[
             pl.BlockSpec(memory_space=pltpu.SMEM),
             pl.BlockSpec(memory_space=pltpu.SMEM),
-            pl.BlockSpec(memory_space=pl.ANY),
+            pl.BlockSpec(memory_space=pltpu.VMEM),
         ],
-        out_specs=pl.BlockSpec(memory_space=pl.ANY),
-        scratch_shapes=[
-            pltpu.VMEM((narrow, UNIT), moved.dtype),
-            pltpu.VMEM((per_group * units, narrow, UNIT), moved.dtype),
-            dma, dma,
-        ],
+        out_specs=pl.BlockSpec(memory_space=pltpu.HBM),
+        scratch_shapes=[pltpu.VMEM((narrow, UNIT), moved.dtype), dma],
+        compiler_params=pltpu.CompilerParams(vmem_limit_bytes=12 * 1024 * 1024),
     )(new_plan, table_rows, moved)
 
 
@@ -787,10 +759,10 @@
     c = lax.axis_index("col")
     chip = g // 2
 
-    def variant(caps):
+    def variant(number, caps):
         slots, room = caps
 
-        def run(old_tables, old_plan, new_plan, marked):
+        def run(old_tables, table_rows, old_plan, new_plan, marked):
             mine = base == chip // over
             n = jnp.arange(slots, dtype=jnp.int32)[:, None]
             inside = (mine & (plane == c))[None, :] & (n >= z_off[None, :]) & (n < (z_off + held)[None, :])
@@ -804,7 +776,10 @@
             inside = (position[None, :] == where) & (e < held[None, :])
             f_pick = jnp.sum(jnp.where(inside, (base * over * room + c_off)[None, :] + e, 0), axis=1)
             picks = jnp.concatenate([z_pick, c_pick, f_pick, slot_of])
-            return move_tables(old_tables, old_plan, new_plan, marked, picks, groups, cols, chunks, caps)
+            moved, pooled = move_tables(
+                old_tables, old_plan, new_plan, marked, picks, groups, cols, chunks, caps, number
+            )
+            return clear_unused(moved, new_plan, table_rows), pooled
 
         return run
 
@@ -812,17 +787,17 @@
     room_full = 2 * per_group * units
     caps = [(full * a // 64, room_full * b // 64) for a, b in SHARES]
     caps = [cap for cap in caps if vmem_bytes(chunks, units, cols, chips, ids.shape[0] * groups * cols, ids.shape[2], cap) < VMEM_ROOM]
-    branches = [variant(cap) for cap in caps]
+    branches = [variant(number, cap) for number, cap in enumerate(caps)]
     if not caps or caps[-1][0] < full:
 
-        def fallback(old_tables, old_plan, new_plan, marked):
-            return move_whole(old_tables, old_plan, new_plan, marked, groups, cols)
+        def fallback(old_tables, table_rows, old_plan, new_plan, marked):
+            moved, pooled = move_whole(old_tables, old_plan, new_plan, marked, groups, cols)
+            return clear_unused(moved, new_plan, table_rows), pooled
 
         branches.append(fallback)
     misfits = (((z_need > cap[0]) | (c_need > cap[1])).astype(jnp.int32) for cap in caps[: len(branches) - 1])
     level = jnp.max(sum(misfits, start=jnp.zeros_like(z_need)))
-    moved, pooled = lax.switch(level, branches, old_tables, old_plan, new_plan, marked)
-    return (clear_unused(moved, new_plan, table_rows), pooled)
+    return lax.switch(level, branches, old_tables, table_rows, old_plan, new_plan, marked)
 
 
 def solution(mesh):

time: 193 us -> 196 us (1.016)
  Pallas kernels: 185 us -> 187 us
    pallas_call x1, Pallas kernels: 178 us -> 183 us  [move_tables(): pl.pallas_call(functools.partial(move_kernel, (groups, cols, units, width...]
    pallas_call x1, Pallas kernels: 6.99 us -> 4.11 us  [clear_unused(): pl.pallas_call(functools.partial(place_kernel, per_group, units), out_sha...]
where the time goes in v1:
time: 196 us; the launch traced here: 195 us
  Pallas kernels  187 us (95%)
  other arithmetic  4.98 us (3%)
    pallas_call x1, Pallas kernels, move_tables(): pl.pallas_call(functools.partial(move_kernel, (groups, cols, units, width...  183 us
    pallas_call x1, Pallas kernels, clear_unused(): pl.pallas_call(functools.partial(place_kernel, per_group, units), out_sha...  4.11 us

profile of v1, /device:TPU:9, one launch (start us, length us, event | category | flops | bytes accessed | tf_op | source)
XLA Modules:
  0.0 195.4 jit_solution(12713507545425085499)
XLA Ops:
  0.7 0.9 select_reduce_fusion.31
  1.6 0.2 select_reduce_fusion.30
  1.8 0.7 fusion.58
  3.1 191.6 %conditional.1 = (f32[8,32,128]{2,1,0:T(8,128)S(1)}, bf16[4,32,32768]{2,1,0:T(8,128)(2,1)}) conditional(s32[]{:T(128)} %clamp.3, (bf16[1,128,32768]{2,1,0:T(8,128)(2,1)}, s32[]{:T(128)}, s32[32]{0:T(128)S(1)}, s32[]{:T(128)}, s32[32]{0:T(128)S(1)}, /*index=5*/s32[32]{0:T(128)S(1)}, s32[32]{0:T(128)S(1)}, ...), branch_computations={%region_6.10_spmd.clone, %region_10.14_spmd.clone, %region_14.18_s... | conditional | flops 119960 | bytes 109901 | solution.py:800
  3.4 0.0 copy-start.3
  3.4 0.0 copy-start.10
  3.4 0.8 select_reduce_fusion.13
  4.3 0.1 select_reduce_fusion.14
  4.4 0.1 select_reduce_fusion.12
  4.5 0.1 select_reduce_fusion.15
  4.6 0.7 pad_add_fusion.3.pick_ref
  5.2 0.9 copy.74
  6.2 1.4 compare_select_fusion.9.ids_ref
  7.6 182.6 %branch_3_fun.2 = (bf16[4,32,32768]{2,1,0:T(8,128)(2,1)S(1)}, f32[8,32,128]{2,1,0:T(8,128)S(1)}) custom-call(s32[32]{0:T(128)} %get-tuple-element.843.old_ref, s32[32]{0:T(128)} %get-tuple-element.841.new_ref.plan_ref, bf16[4,2,16,32768]{3,2,1,0:T(8,128)(2,1)} %bitcast.10, s32[8,32,16]{2,1,0:T(8,128)} %compare_select_fusion.9.ids_ref, s32[344]{0:T(512)} %pad_add_fusion.3.pick_ref), custom_call_target="tpu_custom_call" | custom-call | tf_op jit(solution)/shard_map/cond/branch_3_fun/pallas_call | solution.py:394
  190.2 0.0 copy-done.3
  190.3 0.0 copy-done.10
  190.3 4.1 %branch_3_fun.3 = bf16[4,32,32768]{2,1,0:T(8,128)(2,1)} custom-call(s32[32]{0:T(128)S(1)} %copy-done.3, s32[32]{0:T(128)S(1)} %copy-done.10, bf16[4,32,32768]{2,1,0:T(8,128)(2,1)S(1)} %get-tuple-element.855.moved_ref), custom_call_target="tpu_custom_call" | custom-call | tf_op jit(solution)/shard_map/cond/branch_3_fun/pallas_call | solution.py:707
  194.7 0.7 copy.93
  (11 shorter events, 0.1 us)
Async XLA Ops:
  3.4 186.9 %copy-start.3 = (s32[32]{0:T(128)S(1)}, s32[32]{0:T(128)}, u32[]{:S(2)}) copy-start(s32[32]{0:T(128)} %get-tuple-element.841.new_ref.plan_ref) | copy-start | bytes 388 | tf_op jit(solution)/shard_map/cond
  3.4 186.9 %copy-start.10 = (s32[32]{0:T(128)S(1)}, s32[32]{0:T(128)}, u32[]{:S(2)}) copy-start(s32[32]{0:T(128)} %get-tuple-element.842.rows_ref) | copy-start | bytes 388 | tf_op jit(solution)/shard_map/cond

commit v2 on v1

--- a/solution.py
+++ b/solution.py
@@ -248,7 +248,7 @@
             planes[k][c * slots + n] = spread[k][item, c]
             return carry
 
-        lax.fori_loop(0, slots, one, 0)
+        lax.fori_loop(0, slots, one, 0, unroll=2)
         for d in COLUMN_ORDER(cols):
             column_step(k, d).start()
 
@@ -735,7 +735,7 @@
     units = table_len // UNIT
     chips = groups // 2
     bag_iota = lax.broadcasted_iota(jnp.int32, (1, 1, ids.shape[2]), 2)
-    marked = jnp.where(bag_iota < bag_len[:, :, None], ids, -1)
+    marked = lax.optimization_barrier(jnp.where(bag_iota < bag_len[:, :, None], ids, -1))
     chunks = chunk_list(UNIT, width // cols // NARROW)
 
     over = chunks[0][1]

time: 196 us -> 188 us (0.959)
  Pallas kernels: 187 us -> 180 us
    pallas_call x1, Pallas kernels: 183 us -> 176 us  [move_tables(): pl.pallas_call(functools.partial(move_kernel, (groups, cols, units, width...]
where the time goes in v2:
time: 188 us
  Pallas kernels  180 us (96%)
  other arithmetic  4.32 us (2%)
    pallas_call x1, Pallas kernels, move_tables(): pl.pallas_call(functools.partial(move_kernel, (groups, cols, units, width...  176 us
    pallas_call x1, Pallas kernels, clear_unused(): pl.pallas_call(functools.partial(place_kernel, per_group, units), out_sha...  4.11 us

profile of v2, /device:TPU:9, one launch (start us, length us, event | category | flops | bytes accessed | tf_op | source)
XLA Modules:
  0.0 187.8 jit_solution(8433741059367047387)
XLA Ops:
  0.7 0.9 select_reduce_fusion.31
  1.6 0.2 select_reduce_fusion.30
  1.8 0.7 fusion.59
  3.1 0.9 copy.37
  4.0 0.8 fusion.49
  4.8 182.3 %conditional.1 = (f32[8,32,128]{2,1,0:T(8,128)S(1)}, bf16[4,32,32768]{2,1,0:T(8,128)(2,1)}) conditional(s32[]{:T(128)} %clamp.3, (bf16[1,128,32768]{2,1,0:T(8,128)(2,1)}, s32[]{:T(128)}, s32[32]{0:T(128)S(1)}, s32[]{:T(128)}, s32[32]{0:T(128)S(1)}, /*index=5*/s32[32]{0:T(128)S(1)}, s32[32]{0:T(128)S(1)}, ...), branch_computations={%region_6.10_spmd.clone, %region_10.14_spmd.clone, %region_14.18_s... | conditional | flops 111768 | bytes 26953 | solution.py:800
  5.1 0.0 copy-start.2
  5.1 0.0 copy-start.9
  5.1 0.8 select_reduce_fusion.9
  6.0 0.1 select_reduce_fusion.10
  6.1 0.1 select_reduce_fusion.8
  6.2 0.1 select_reduce_fusion.11
  6.3 0.7 pad_add_fusion.2.pick_ref
  6.9 175.6 %branch_2_fun.2 = (bf16[4,32,32768]{2,1,0:T(8,128)(2,1)S(1)}, f32[8,32,128]{2,1,0:T(8,128)S(1)}) custom-call(s32[32]{0:T(128)} %get-tuple-element.687.old_ref, s32[32]{0:T(128)} %get-tuple-element.685.new_ref.plan_ref, bf16[4,2,16,32768]{3,2,1,0:T(8,128)(2,1)} %bitcast.9, s32[8,32,16]{2,1,0:T(8,128)S(1)} %get-tuple-element.688.ids_ref, ...), custom_call_target="tpu_custom_call" | custom-call | tf_op jit(solution)/shard_map/cond/branch_2_fun/pallas_call | solution.py:394
  182.5 0.0 copy-done.2
  182.5 0.0 copy-done.9
  182.5 4.1 %branch_2_fun.3 = bf16[4,32,32768]{2,1,0:T(8,128)(2,1)} custom-call(s32[32]{0:T(128)S(1)} %copy-done.2, s32[32]{0:T(128)S(1)} %copy-done.9, bf16[4,32,32768]{2,1,0:T(8,128)(2,1)S(1)} %get-tuple-element.700.moved_ref), custom_call_target="tpu_custom_call" | custom-call | tf_op jit(solution)/shard_map/cond/branch_2_fun/pallas_call | solution.py:707
  187.2 0.7 copy.53
  (10 shorter events, 0.1 us)
Async XLA Ops:
  5.1 177.4 %copy-start.2 = (s32[32]{0:T(128)S(1)}, s32[32]{0:T(128)}, u32[]{:S(2)}) copy-start(s32[32]{0:T(128)} %get-tuple-element.685.new_ref.plan_ref) | copy-start | bytes 388 | tf_op jit(solution)/shard_map/cond
  5.1 177.4 %copy-start.9 = (s32[32]{0:T(128)S(1)}, s32[32]{0:T(128)}, u32[]{:S(2)}) copy-start(s32[32]{0:T(128)} %get-tuple-element.686.rows_ref) | copy-start | bytes 388 | tf_op jit(solution)/shard_map/cond
